TPU v7x, 32 devices: a whole 2x2x4 slice. The times are simulated.
32 devices in a mesh: dp: 8 (over z, x), cent: 4 (over y, core).
Axes of the slice: x: 2, y: 2, z: 4, core: 2. Of those that a mesh axis runs over, the one named last changes fastest.
Arguments:
- documents: bfloat16 [16384, 2048], P(('dp', 'cent')), may hold values from -6 to 6
- assigned: int32 [16384], P(('dp', 'cent')), may hold values from 0 to 12287, as said below
- centroids: bfloat16 [12288, 2048], P(('dp', 'cent')), may hold values from -6 to 6
- owner_slot: int32 [12288], replicated, may hold values from 0 to 12287, as said below
Outputs:
- prototypicality: float32 [16384], P(('dp', 'cent'))
- redundancy: float32 [16384], P(('dp', 'cent'))
- cluster_stats: float32 [3, 12288], P(None, ('dp', 'cent'))
Inputs may be any that keep to these rules, and one draw needn't show every extreme that they name: `owner_slot`: A permutation of the cluster numbers. `assigned`: of the 512 documents of one device, at most 32 have a slot in any one owner's block of 384 slots, and at most 80 have slots with the owners that share one dp index; in every draw some device reaches 80, and one owner receives exactly 32 from every device.
All inputs are finite; a program needn't handle non-finite values.
Results may differ from a plain program's by a relative error of at most 0.0003.
Values may be sent and summed in bfloat16 or wider, within the bound.
A program may use at most 64 MiB of HBM per device.

v0:
```python
import math

import jax
import jax.numpy as jnp
from jax import lax
from jax.sharding import PartitionSpec as P


def bucket_positions(target, groups, capacity):
    length = target.shape[0]
    indicator = (target[:, None] == jnp.arange(groups, dtype=jnp.int32)[None, :]).astype(
        jnp.bfloat16
    )
    earlier = (
        lax.broadcasted_iota(jnp.int32, (length, length), 0)
        > lax.broadcasted_iota(jnp.int32, (length, length), 1)
    ).astype(jnp.bfloat16)
    before = jnp.dot(earlier, indicator, preferred_element_type=jnp.float32)
    rank_ids = jnp.sum(before * indicator.astype(jnp.float32), axis=1).astype(jnp.int32)
    return jnp.where(target < groups, target * capacity + rank_ids, groups * capacity)


def owner_work(incoming, incoming_tags, centroids):
    table_rows = centroids.shape[0]
    width = incoming.shape[1]
    length = incoming_tags.shape[0]
    is_live = incoming_tags >= 0
    safe_slot = jnp.clip(incoming_tags, 0, table_rows - 1)
    cent_sq = jnp.einsum("kd,kd->k", centroids, centroids, preferred_element_type=jnp.float32)
    cent_vec = centroids[safe_slot]
    cross_dot = jnp.einsum("sd,sd->s", incoming, cent_vec, preferred_element_type=jnp.float32)
    self_sq = jnp.einsum("sd,sd->s", incoming, incoming, preferred_element_type=jnp.float32)
    inverse_norm = lax.rsqrt(self_sq + 1.0)
    similarity = cross_dot * inverse_norm * lax.rsqrt(cent_sq[safe_slot] + 1.0)
    members = (incoming_tags[:, None] == jnp.arange(table_rows, dtype=jnp.int32)[None, :]).astype(
        jnp.float32
    )
    live_weight = is_live.astype(jnp.float32)
    moments = jnp.stack(
        [live_weight, live_weight * similarity, live_weight * similarity * similarity]
    )
    cluster_totals = jnp.dot(
        moments, members, precision=lax.Precision.HIGHEST, preferred_element_type=jnp.float32
    )
    count_floor = jnp.maximum(cluster_totals[0], 1.0)
    mean_sim = cluster_totals[1] / count_floor
    variance = jnp.maximum(cluster_totals[2] / count_floor - mean_sim * mean_sim, 0.0)
    proto_score = jnp.where(
        is_live,
        (mean_sim[safe_slot] - similarity) / jnp.sqrt(variance[safe_slot] + 1.0 / width),
        0.0,
    )
    gram_block = lax.dot_general(
        incoming, incoming, (((1,), (1,)), ((), ())), preferred_element_type=jnp.float32
    )
    cosine = gram_block * inverse_norm[:, None] * inverse_norm[None, :]
    not_self = lax.broadcasted_iota(jnp.int32, (length, length), 0) != lax.broadcasted_iota(
        jnp.int32, (length, length), 1
    )
    same_cluster = (incoming_tags[:, None] == incoming_tags[None, :]) & is_live[:, None] & not_self
    redundant = math.sqrt(width) * jnp.max(jnp.where(same_cluster, cosine, 0.0), axis=1)
    return (cluster_totals, proto_score, redundant)


def local(documents, assigned, centroids, owner_slot):
    doc_count, width = documents.shape
    table_rows = centroids.shape[0]
    dp_count = lax.axis_size("dp")
    cent_count = lax.axis_size("cent")
    owner_count = dp_count * cent_count
    pair_cap = 2 * doc_count // owner_count
    row_cap = 5 * cent_count * pair_cap // 8
    slot_ids = owner_slot[assigned]
    owner_ids = slot_ids // table_rows
    local_ids = slot_ids % table_rows
    row_ids = owner_ids // cent_count
    col_ids = owner_ids % cent_count
    first_pos = bucket_positions(row_ids, dp_count, row_cap)
    outgoing = jnp.zeros((dp_count * row_cap, width), jnp.bfloat16).at[first_pos].set(documents)
    tag_ids = (
        jnp.full((dp_count * row_cap,), -1, jnp.int32)
        .at[first_pos]
        .set(col_ids * table_rows + local_ids)
    )
    relayed, relayed_tags = (
        lax.all_to_all(
            outgoing.reshape(dp_count, row_cap, width),
            "dp",
            split_axis=0,
            concat_axis=0,
            tiled=True,
        ),
        lax.all_to_all(
            tag_ids.reshape(dp_count, row_cap), "dp", split_axis=0, concat_axis=0, tiled=True
        ),
    )
    relayed = relayed.reshape(-1, width)
    relayed_tags = relayed_tags.reshape(-1)
    relay_live = relayed_tags >= 0
    relay_target = jnp.where(relay_live, relayed_tags // table_rows, cent_count)
    inner_cap = dp_count * pair_cap
    second_pos = bucket_positions(relay_target, cent_count, inner_cap)
    forward = (
        jnp.zeros((cent_count * inner_cap, width), jnp.bfloat16)
        .at[second_pos]
        .set(relayed, mode="drop")
    )
    forward_tags = (
        jnp.full((cent_count * inner_cap,), -1, jnp.int32)
        .at[second_pos]
        .set(jnp.where(relay_live, relayed_tags % table_rows, -1), mode="drop")
    )
    incoming, incoming_tags = (
        lax.all_to_all(
            forward.reshape(cent_count, inner_cap, width),
            "cent",
            split_axis=0,
            concat_axis=0,
            tiled=True,
        ),
        lax.all_to_all(
            forward_tags.reshape(cent_count, inner_cap),
            "cent",
            split_axis=0,
            concat_axis=0,
            tiled=True,
        ),
    )
    cluster_totals, proto_score, redundant = owner_work(
        incoming.reshape(-1, width), incoming_tags.reshape(-1), centroids
    )
    back_score, back_redundant = (
        lax.all_to_all(
            proto_score.reshape(cent_count, inner_cap),
            "cent",
            split_axis=0,
            concat_axis=0,
            tiled=True,
        ),
        lax.all_to_all(
            redundant.reshape(cent_count, inner_cap),
            "cent",
            split_axis=0,
            concat_axis=0,
            tiled=True,
        ),
    )
    safe_pos = jnp.clip(second_pos, 0, cent_count * inner_cap - 1)
    relay_score = jnp.where(relay_live, back_score.reshape(-1)[safe_pos], 0.0)
    relay_redundant = jnp.where(relay_live, back_redundant.reshape(-1)[safe_pos], 0.0)
    home_score, home_redundant = (
        lax.all_to_all(
            relay_score.reshape(dp_count, row_cap), "dp", split_axis=0, concat_axis=0, tiled=True
        ),
        lax.all_to_all(
            relay_redundant.reshape(dp_count, row_cap),
            "dp",
            split_axis=0,
            concat_axis=0,
            tiled=True,
        ),
    )
    prototypicality = home_score.reshape(-1)[first_pos]
    redundancy = home_redundant.reshape(-1)[first_pos]
    return (prototypicality, redundancy, cluster_totals)


def solution(mesh):
    in_specs = (P(("dp", "cent"), None), P(("dp", "cent")), P(("dp", "cent"), None), P())
    out_specs = (P(("dp", "cent")), P(("dp", "cent")), P(None, ("dp", "cent")))
    return jax.shard_map(local, mesh=mesh, in_specs=in_specs, out_specs=out_specs, check_vma=False)
```

profile of v0, /device:TPU:0, one launch (start us, length us, event | category | flops | bytes accessed | tf_op | source)
XLA Modules:
  0.0 223.4 jit_solution(2602086544117102727)
XLA Ops:
  0.6 0.7 compare_select_fusion.6
  1.4 3.1 %gather_fusion = s32[512]{0:T(512)S(1)} fusion(s32[12288]{0:T(1024)S(1)} %copy-done, s32[1024]{0:T(1024)S(1)} %pad_clamp_fusion.2), kind=kCustom, calls=%fused_computation | custom fusion | bytes 6144 | tf_op jit(solution)/shard_map/gather | solution.py:73
  4.9 2.4 %scatter_custom_fusion = s32[640]{0:T(1024)S(1)} fusion(s32[512]{0:T(512)S(1)} %bitcast.33, s32[512]{0:T(512)S(1)} %get-tuple-element.17, s32[]{:T(128)} %constant.35.clone.1), kind=kCustom, calls=%fused_computation.101 | custom fusion | bytes 2564 | tf_op jit(solution)/shard_map/scatter | solution.py:83
  7.4 0.7 all_to_all.36
  8.1 7.3 %all-to-all-start = ((s32[8,1,80]{2,1,0:T(1,128)}), s32[8,1,80]{2,1,0:T(1,128)S(1)}, u32[]{:S(2)}, u32[]{:S(2)}) async-start(s32[8,1,80]{2,1,0:T(1,128)} %all_to_all.36), calls=%async_computation | async-start | bytes 8192 | tf_op jit(solution)/shard_map/all_to_all | solution.py:93
  15.3 6.4 %scatter_custom_fusion.2 = bf16[640,2048]{1,0:T(8,128)(2,1)} fusion(s32[512]{0:T(512)S(1)} %bitcast.34, bf16[512,2048]{1,0:T(8,128)(2,1)} %param.4, bf16[]{:T(256)} %constant.88.clone.1), kind=kCustom, calls=%fused_computation.28 | custom fusion | bytes 2621952 | tf_op jit(solution)/shard_map/scatter | solution.py:79
  21.8 6.0 %all-to-all-start.2 = ((bf16[8,80,2048]{2,1,0:T(8,128)(2,1)}), bf16[8,80,2048]{2,1,0:T(8,128)(2,1)S(1)}, u32[]{:S(2)}, u32[]{:S(2)}) async-start(bf16[8,80,2048]{2,1,0:T(8,128)(2,1)} %bitcast.6), calls=%async_computation.2 | async-start | bytes 5242880 | tf_op jit(solution)/shard_map/all_to_all | solution.py:86
  28.5 0.7 fusion.41
  30.0 4.7 %scatter_custom_fusion.1 = s32[1024]{0:T(1024)} fusion(s32[640]{0:T(1024)S(1)} %get-tuple-element.11, s32[640]{0:T(1024)S(1)} %get-tuple-element.19, s32[]{:T(128)} %constant.35.clone.1), kind=kCustom, calls=%fused_computation.96 | custom fusion | bytes 4100 | tf_op jit(solution)/shard_map/scatter | solution.py:111
  34.7 52.0 %all-to-all-done.2 = bf16[8,80,2048]{2,1,0:T(8,128)(2,1)S(1)} async-done(((bf16[8,80,2048]{2,1,0:T(8,128)(2,1)}), bf16[8,80,2048]{2,1,0:T(8,128)(2,1)S(1)}, u32[]{:S(2)}, u32[]{:S(2)}) %all-to-all-start.2) | async-done | bytes 2621472 | tf_op jit(solution)/shard_map/all_to_all | solution.py:86
  86.7 3.4 %all-to-all-start.1 = ((s32[4,1,256]{2,1,0:T(1,128)}), s32[4,1,256]{2,1,0:T(1,128)S(1)}, u32[]{:S(2)}, u32[]{:S(2)}) async-start(s32[4,1,256]{2,1,0:T(1,128)} %bitcast.3), calls=%async_computation.1 | async-start | bytes 8192 | tf_op jit(solution)/shard_map/all_to_all | solution.py:121
  90.1 9.4 %scatter_custom_fusion.3 = bf16[1024,2048]{1,0:T(8,128)(2,1)} fusion(s32[640]{0:T(1024)S(1)} %get-tuple-element.11, bf16[640,2048]{1,0:T(8,128)(2,1)S(1)} %bitcast.26, bf16[]{:T(256)} %constant.88.clone.1), kind=kCustom, calls=%fused_computation.22 | custom fusion | bytes 4194306 | tf_op jit(solution)/shard_map/scatter | solution.py:106
  99.5 5.0 %all-to-all-start.3 = ((bf16[4,256,2048]{2,1,0:T(8,128)(2,1)}), bf16[4,256,2048]{2,1,0:T(8,128)(2,1)}, u32[]{:S(2)}, u32[]{:S(2)}) async-start(bf16[4,256,2048]{2,1,0:T(8,128)(2,1)} %bitcast.25), calls=%async_computation.3 | async-start | bytes 8388608 | tf_op jit(solution)/shard_map/all_to_all | solution.py:114
  105.0 6.1 %gather_fusion.1 = bf16[1024,2048]{1,0:T(8,128)(2,1)} fusion(bf16[384,2048]{1,0:T(8,128)(2,1)S(1)} %copy-done.1, s32[1024]{0:T(1024)S(1)} %broadcast_clamp_fusion), kind=kCustom, calls=%fused_computation.1 | custom fusion | bytes 8392704 | tf_op jit(solution)/shard_map/gather | solution.py:30
  111.0 6.9 %gather_fusion.2 = f32[1024]{0:T(1024)S(1)} fusion(f32[384]{0:T(512)S(1)} %fusion.3, s32[1024]{0:T(1024)S(1)} %broadcast_clamp_fusion), kind=kCustom, calls=%fused_computation.2 | custom fusion | bytes 12288 | tf_op jit(solution)/shard_map/gather | solution.py:34
  117.9 34.8 %all-to-all-done.3 = bf16[4,256,2048]{2,1,0:T(8,128)(2,1)} async-done(((bf16[4,256,2048]{2,1,0:T(8,128)(2,1)}), bf16[4,256,2048]{2,1,0:T(8,128)(2,1)}, u32[]{:S(2)}, u32[]{:S(2)}) %all-to-all-start.3) | async-done | bytes 4194336 | tf_op jit(solution)/shard_map/all_to_all | solution.py:114
  152.7 5.2 %fusion.1 = (f32[1024]{0:T(1024)S(1)}, f32[1024]{0:T(1024)S(1)}) fusion(bf16[4,256,2048]{2,1,0:T(8,128)(2,1)} %all-to-all-done.3, bf16[1024,2048]{1,0:T(8,128)(2,1)} %gather_fusion.1), kind=kLoop, calls=%fused_computation.16 | loop fusion | flops 12580864 | bytes 8396800 | tf_op jit(solution)/shard_map/sd,sd->s/dot_general | solution.py:32
  158.0 0.7 fusion.7
  158.7 6.9 %gather_fusion.3 = f32[1024]{0:T(1024)S(1)} fusion(f32[384]{0:T(512)S(1)} %get-tuple-element.5, s32[1024]{0:T(1024)S(1)} %broadcast_clamp_fusion), kind=kCustom, calls=%fused_computation.3 | custom fusion | bytes 12288 | tf_op jit(solution)/shard_map/gather | solution.py:50
  165.6 6.9 %gather_fusion.4 = f32[1024]{0:T(1024)S(1)} fusion(f32[384]{0:T(512)S(1)} %subtract_maximum_fusion, s32[1024]{0:T(1024)S(1)} %broadcast_clamp_fusion), kind=kCustom, calls=%fused_computation.4 | custom fusion | bytes 12288 | tf_op jit(solution)/shard_map/gather | solution.py:50
  173.0 3.4 %all-to-all-start.4 = ((f32[4,1,256]{2,1,0:T(1,128)}), f32[4,1,256]{2,1,0:T(1,128)S(1)}, u32[]{:S(2)}, u32[]{:S(2)}) async-start(f32[4,1,256]{2,1,0:T(1,128)} %bitcast.14), calls=%async_computation.4 | async-start | bytes 8192 | tf_op jit(solution)/shard_map/all_to_all | solution.py:133
  176.5 8.5 %select_reduce_fusion = f32[1024]{0:T(1024)S(1)} fusion(bf16[1024,2048]{1,0:T(8,128)(2,1)} %bitcast.9, f32[1024]{0:T(1024)S(1)} %get-tuple-element.23, s32[1024]{0:T(1024)S(1)} %bitcast.29, pred[1024]{0:T(1024)(128)(4,1)S(1)} %get-tuple-element.14), kind=kOutput, calls=%fused_computation.17 | convolution fusion | flops 4303354880 | bytes 4207616 | tf_op jit(solution)/shard_map/dot_general | solution.py:53
  185.6 3.2 %all-to-all-start.6 = ((f32[4,1,256]{2,1,0:T(1,128)}), f32[4,1,256]{2,1,0:T(1,128)S(1)}, u32[]{:S(2)}, u32[]{:S(2)}) async-start(f32[4,1,256]{2,1,0:T(1,128)} %bitcast.16), calls=%async_computation.6 | async-start | bytes 8192 | tf_op jit(solution)/shard_map/all_to_all | solution.py:140
  188.9 2.8 %gather_fusion.5 = f32[640]{0:T(1024)S(1)} fusion(f32[1024]{0:T(1024)S(1)} %bitcast.23, s32[1024]{0:T(1024)S(1)} %pad_clamp_fusion.1), kind=kCustom, calls=%fused_computation.5 | custom fusion | bytes 7680 | tf_op jit(solution)/shard_map/gather | solution.py:149
  191.8 0.9 all-to-all-done.6
  192.7 2.8 %gather_fusion.7 = f32[640]{0:T(1024)S(1)} fusion(f32[1024]{0:T(1024)S(1)} %bitcast.24, s32[1024]{0:T(1024)S(1)} %pad_clamp_fusion.1), kind=kCustom, calls=%fused_computation.7 | custom fusion | bytes 7680 | tf_op jit(solution)/shard_map/gather | solution.py:150
  196.1 9.9 %all_to_all.55 = f32[8,1,80]{2,1,0:T(1,128)S(1)} all-to-all(f32[8,1,80]{2,1,0:T(1,128)S(1)} %get-tuple-element.21), channel_id=1, replica_groups=mesh['dp'=8,'cent'=4] {'dp'}, dimensions={0} | all-to-all | bytes 5120 | tf_op jit(solution)/shard_map/all_to_all | solution.py:155
  206.1 3.3 %all-to-all-start.5 = ((f32[8,1,80]{2,1,0:T(1,128)}), f32[8,1,80]{2,1,0:T(1,128)S(1)}, u32[]{:S(2)}, u32[]{:S(2)}) async-start(f32[8,1,80]{2,1,0:T(1,128)} %get-tuple-element.22), calls=%async_computation.5 | async-start | bytes 8192 | tf_op jit(solution)/shard_map/all_to_all | solution.py:152
  210.7 5.2 %all-to-all-done.5 = f32[8,1,80]{2,1,0:T(1,128)S(1)} async-done(((f32[8,1,80]{2,1,0:T(1,128)}), f32[8,1,80]{2,1,0:T(1,128)S(1)}, u32[]{:S(2)}, u32[]{:S(2)}) %all-to-all-start.5) | async-done | bytes 2592 | tf_op jit(solution)/shard_map/all_to_all | solution.py:152
  215.8 0.7 reduce.37
  216.6 3.4 %gather_fusion.8 = f32[512]{0:T(512)} fusion(f32[640]{0:T(1024)S(1)} %reshape.403, s32[1024]{0:T(1024)S(1)} %pad_clamp_fusion), kind=kCustom, calls=%fused_computation.8 | custom fusion | bytes 6144 | tf_op jit(solution)/shard_map/gather | solution.py:164
  220.0 3.4 %gather_fusion.6 = f32[512]{0:T(512)} fusion(f32[640]{0:T(1024)S(1)} %reshape.401, s32[1024]{0:T(1024)S(1)} %pad_clamp_fusion), kind=kCustom, calls=%fused_computation.6 | custom fusion | bytes 6144 | tf_op jit(solution)/shard_map/gather | solution.py:163
  (48 shorter events, 5.7 us)
Async XLA Ops:
  0.6 0.8 copy-start
  8.1 13.7 %all-to-all-start = ((s32[8,1,80]{2,1,0:T(1,128)}), s32[8,1,80]{2,1,0:T(1,128)S(1)}, u32[]{:S(2)}, u32[]{:S(2)}) async-start(s32[8,1,80]{2,1,0:T(1,128)} %all_to_all.36), calls=%async_computation | async-start | bytes 8192 | tf_op jit(solution)/shard_map/all_to_all | solution.py:93
  21.8 64.9 %all-to-all-start.2 = ((bf16[8,80,2048]{2,1,0:T(8,128)(2,1)}), bf16[8,80,2048]{2,1,0:T(8,128)(2,1)S(1)}, u32[]{:S(2)}, u32[]{:S(2)}) async-start(bf16[8,80,2048]{2,1,0:T(8,128)(2,1)} %bitcast.6), calls=%async_computation.2 | async-start | bytes 5242880 | tf_op jit(solution)/shard_map/all_to_all | solution.py:86
  86.7 12.8 %all-to-all-start.1 = ((s32[4,1,256]{2,1,0:T(1,128)}), s32[4,1,256]{2,1,0:T(1,128)S(1)}, u32[]{:S(2)}, u32[]{:S(2)}) async-start(s32[4,1,256]{2,1,0:T(1,128)} %bitcast.3), calls=%async_computation.1 | async-start | bytes 8192 | tf_op jit(solution)/shard_map/all_to_all | solution.py:121
  99.5 5.0 %copy-start.1 = (bf16[384,2048]{1,0:T(8,128)(2,1)S(1)}, bf16[384,2048]{1,0:T(8,128)(2,1)}, u32[]{:S(2)}) copy-start(bf16[384,2048]{1,0:T(8,128)(2,1)} %param.6) | copy-start | bytes 4718596
  99.5 53.2 %all-to-all-start.3 = ((bf16[4,256,2048]{2,1,0:T(8,128)(2,1)}), bf16[4,256,2048]{2,1,0:T(8,128)(2,1)}, u32[]{:S(2)}, u32[]{:S(2)}) async-start(bf16[4,256,2048]{2,1,0:T(8,128)(2,1)} %bitcast.25), calls=%async_computation.3 | async-start | bytes 8388608 | tf_op jit(solution)/shard_map/all_to_all | solution.py:114
  158.6 13.8 %copy-start.2 = (f32[3,384]{1,0:T(4,128)}, f32[3,384]{1,0:T(4,128)S(1)}, u32[]{:S(2)}) copy-start(f32[3,384]{1,0:T(4,128)S(1)} %fusion.7) | copy-start | bytes 13828
  173.0 12.6 %all-to-all-start.4 = ((f32[4,1,256]{2,1,0:T(1,128)}), f32[4,1,256]{2,1,0:T(1,128)S(1)}, u32[]{:S(2)}, u32[]{:S(2)}) async-start(f32[4,1,256]{2,1,0:T(1,128)} %bitcast.14), calls=%async_computation.4 | async-start | bytes 8192 | tf_op jit(solution)/shard_map/all_to_all | solution.py:133
  185.6 7.0 %all-to-all-start.6 = ((f32[4,1,256]{2,1,0:T(1,128)}), f32[4,1,256]{2,1,0:T(1,128)S(1)}, u32[]{:S(2)}, u32[]{:S(2)}) async-start(f32[4,1,256]{2,1,0:T(1,128)} %bitcast.16), calls=%async_computation.6 | async-start | bytes 8192 | tf_op jit(solution)/shard_map/all_to_all | solution.py:140
  206.1 9.8 %all-to-all-start.5 = ((f32[8,1,80]{2,1,0:T(1,128)}), f32[8,1,80]{2,1,0:T(1,128)S(1)}, u32[]{:S(2)}, u32[]{:S(2)}) async-start(f32[8,1,80]{2,1,0:T(1,128)} %get-tuple-element.22), calls=%async_computation.5 | async-start | bytes 8192 | tf_op jit(solution)/shard_map/all_to_all | solution.py:152
where the time goes:
time: 224 us; the launch traced here: 223 us
  waiting for transfers between devices  92.9 us (41%)
  local copies, waits for them, and re-layouts  67.8 us (30%)
  starting transfers between devices  31.7 us (14%)
  other arithmetic  10.4 us (5%)
  blocking collectives  9.92 us (4%)
  matrix products  9.77 us (4%)
    all_to_all x1, waiting for transfers between devices, local(): lax.all_to_all(outgoing.reshape(dp_count, row_cap, width), 'dp', split_ax...  52 us
    all_to_all x1, waiting for transfers between devices, local(): lax.all_to_all(forward.reshape(cent_count, inner_cap, width), 'cent', spl...  34.8 us
    all_to_all x1, blocking collectives, local(): lax.all_to_all(relay_redundant.reshape(dp_count, row_cap), 'dp', split_ax...  9.92 us
    scatter x1, local copies, waits for them, and re-layouts, local(): forward = jnp.zeros((cent_count * inner_cap, width), jnp.bfloat16).at[sec...  9.4 us
    dot_general x1, matrix products, owner_work(): lax.dot_general(incoming, incoming, (((1,), (1,)), ((), ())), preferred_e...  8.54 us
    all_to_all x1, starting transfers between devices, local(): lax.all_to_all(tag_ids.reshape(dp_count, row_cap), 'dp', split_axis=0, co...  7.28 us
    gather x1, local copies, waits for them, and re-layouts, owner_work(): mean_sim[safe_slot] - similarity  6.87 us
    gather x1, local copies, waits for them, and re-layouts, owner_work(): variance[safe_slot] + 1.0 / width  6.87 us
  transfers between devices with their start and end apart: 7, of which 4 were waited for; matrix products, arithmetic and copies ran while one was open for 22% of the time, Pallas kernels for 0%

commit v1 on v0

v1 whole, which is shorter than its diff:
```python
import functools
import math

import jax
import jax.numpy as jnp
from jax import lax
from jax.experimental import pallas as pl
from jax.experimental.pallas import tpu as pltpu
from jax.sharding import PartitionSpec as P

F32 = jnp.float32
BF16 = jnp.bfloat16
HIGH = lax.Precision.HIGHEST
LANES = 128
SUB = 8


def round_up(value, unit):
    return -(-value // unit) * unit


def exclusive_or(left, right, extent):
    total = 0
    bit = 1
    while bit < extent:
        total = total + lax.rem(lax.rem(lax.div(left, bit), 2) + lax.rem(lax.div(right, bit), 2), 2) * bit
        bit *= 2
    return total


def iota(shape, dim):
    return lax.broadcasted_iota(jnp.int32, shape, dim)


def mm(left, right):
    return lax.dot_general(left, right, (((1,), (0,)), ((), ())), preferred_element_type=F32)


def mm_t(left, right):
    return lax.dot_general(left, right, (((1,), (1,)), ((), ())), preferred_element_type=F32)


def one_hot(condition):
    return jnp.where(condition, 1.0, 0.0).astype(BF16)


def kernel(
    dims,
    docs_ref,
    assigned_ref,
    cent_ref,
    table_ref,
    proto_ref,
    red_ref,
    stats_ref,
    send_buf,
    chunk_buf,
    code_send,
    code_recv,
    fwd_buf,
    rows_buf,
    tbl_send,
    tbl_recv,
    res_send,
    res_recv,
    pos_buf,
    tag_col,
    tag_row,
    inv_col,
    inv_row,
    sim_col,
    best_row,
    a_send,
    a_recv,
    m_send,
    m_recv,
    f_send,
    f_recv,
    t_send,
    t_recv,
    r_send,
    r_recv,
):
    R, C, K, Q = dims
    O = R * C
    CK = C * K
    L, D = docs_ref.shape
    S = cent_ref.shape[0]
    T = table_ref.shape[0]
    row_me = lax.axis_index("dp")
    col_me = lax.axis_index("cent")
    own = row_me * C + col_me

    def peer(q):
        step = lax.div(q, C)
        return step, exclusive_or(row_me, step, R), lax.rem(col_me + lax.rem(q, C), C)

    def where_is(r, c):
        return {"dp": r, "cent": c}

    def remote(src, dst, send, recv, r, c):
        return pltpu.make_async_remote_copy(
            src_ref=src,
            dst_ref=dst,
            send_sem=send,
            recv_sem=recv,
            device_id=where_is(r, c),
            device_id_type=pl.DeviceIdType.MESH,
        )

    barrier = pltpu.get_barrier_semaphore()

    def greet(q, carry):
        _, r, c = peer(q)
        pl.semaphore_signal(
            barrier, inc=1, device_id=where_is(r, c), device_id_type=pl.DeviceIdType.MESH
        )
        return carry

    lax.fori_loop(1, O, greet, 0)

    assigned = assigned_ref[...]
    high = lax.shift_right_logical(assigned, 7)
    low = jnp.bitwise_and(assigned, 127)
    table = table_ref[...]
    d0 = jnp.bitwise_and(table, 127)
    d1 = jnp.bitwise_and(lax.shift_right_logical(table, 7), 127)
    d2 = lax.shift_right_logical(table, 14)
    pick = one_hot(iota((T, L), 0) == high)

    def look(digit):
        return lax.dot_general(
            digit.astype(F32).astype(BF16), pick, (((0,), (0,)), ((), ())), preferred_element_type=F32
        )

    looked = look(d0) + 128.0 * look(d1) + 16384.0 * look(d2)
    slot = jnp.sum(jnp.where(iota((LANES, L), 0) == low, looked, 0.0), axis=0, keepdims=True)
    owner = jnp.floor((slot + 0.5) * (1.0 / S))
    local_id = slot - owner * S
    row = jnp.floor((owner + 0.5) * (1.0 / C))
    owner_i = owner.astype(jnp.int32)
    row_i = row.astype(jnp.int32)
    is_owner = jnp.where(iota((O, L), 0) == owner_i, 1.0, 0.0)
    is_row = jnp.where(iota((R, L), 0) == row_i, 1.0, 0.0)
    earlier = one_hot(iota((L, L), 0) < iota((L, L), 1))
    rank_owner = jnp.sum(mm(is_owner.astype(BF16), earlier) * is_owner, axis=0, keepdims=True)
    rank_row = jnp.sum(mm(is_row.astype(BF16), earlier) * is_row, axis=0, keepdims=True)
    position = (row * Q + rank_row).astype(jnp.int32)
    code = ((owner - row * C) * K + rank_owner + 1.0).astype(BF16)
    code8 = jnp.broadcast_to(code, (SUB, L))
    rank_i = rank_owner.astype(jnp.int32)
    pos_buf[...] = jnp.broadcast_to(position, (SUB, L))

    is_owner8 = lax.shift_right_logical(iota((O * SUB, L), 0), 3) == owner_i
    is_rank = one_hot(iota((LANES, L), 0) == rank_i)
    tag = local_id + 1.0
    tag_hi = jnp.floor(tag * (1.0 / 128.0))
    tag_lo = tag - tag_hi * 128.0
    tags = 128.0 * mm_t(jnp.where(is_owner8, tag_hi, 0.0).astype(BF16), is_rank) + mm_t(
        jnp.where(is_owner8, tag_lo, 0.0).astype(BF16), is_rank
    )
    tbl_send[...] = tags.reshape(O, SUB, LANES)

    pl.semaphore_wait(barrier, O - 1)

    def send_copy(t):
        r = exclusive_or(row_me, t, R)
        return (
            remote(send_buf.at[t], chunk_buf.at[t], a_send.at[t], a_recv.at[t], r, col_me),
            remote(code_send.at[t], code_recv.at[t], m_send.at[t], m_recv.at[t], r, col_me),
        )

    def bucket(t):
        r = exclusive_or(row_me, t, R)
        choose = one_hot(iota((Q, L), 0) + r * Q == pos_buf[0:1, :])
        return mm(choose, docs_ref[...]).astype(BF16), mm_t(code8, choose)

    def ship(t, carry):
        packed, codes = bucket(t)
        send_buf[t] = packed
        code_send[t] = codes
        for copy in send_copy(t):
            copy.start()
        return carry

    lax.fori_loop(1, R, ship, 0)
    packed, codes = bucket(0)
    chunk_buf[0] = packed
    code_recv[0] = codes

    def tbl_copy(q):
        t, r, c = peer(q)
        return remote(
            tbl_send.at[r * C + c], tbl_recv.at[t * C + col_me], t_send.at[q], t_recv.at[t * C + col_me], r, c
        )

    def tbl_arrival(q):
        t, r, c = peer(q)
        return remote(
            tbl_send.at[r * C + c], tbl_recv.at[t * C + c], t_send.at[q], t_recv.at[t * C + c], r, c
        )

    def start_tbl(q, carry):
        tbl_copy(q).start()
        return carry

    lax.fori_loop(1, O, start_tbl, 0)
    tbl_recv[col_me] = tbl_send[own]

    cent_sq = jnp.zeros((SUB, S), F32)
    ones = jnp.ones((SUB, 256), F32)

    squares = []
    for part in range(0, D, 256):
        block = cent_ref[:, part : part + 256].astype(F32)
        squares.append(block * block)
    while len(squares) > 1:
        squares = [a + b for a, b in zip(squares[::2], squares[1::2])] + (
            [squares[-1]] if len(squares) % 2 else []
        )
    cent_sq = lax.dot_general(
        ones, squares[0], (((1,), (1,)), ((), ())), precision=HIGH, preferred_element_type=F32
    )
    cent_inv = lax.rsqrt(cent_sq[0:1, :] + 1.0)

    def wait_tbl(q, carry):
        tbl_arrival(q).wait_recv()
        return carry

    lax.fori_loop(1, O, wait_tbl, 0)

    eye = iota((CK, CK), 0) == iota((CK, CK), 1)

    def spread(t, carry):
        column = jnp.zeros((CK, 1), F32)
        for c in range(C):
            line = tbl_recv[t * C + c][0:1, :]
            here = iota((CK, LANES), 0) - c * K == iota((CK, LANES), 1)
            here = here & (iota((CK, LANES), 1) < K)
            column = column + jnp.sum(jnp.where(here, line, 0.0), axis=1, keepdims=True)
        tag_col[t] = column
        flat = jnp.sum(jnp.where(eye, column, 0.0), axis=0, keepdims=True)
        tag_row[t] = jnp.where(flat > 0.0, flat, -1.0)
        return carry

    lax.fori_loop(0, R, spread, 0)

    stats_ref[...] = jnp.zeros(stats_ref.shape, F32)

    def fwd_copy(t, c):
        return remote(
            fwd_buf.at[t, c], rows_buf.at[t, col_me], f_send.at[t, c], f_recv.at[t, col_me], row_me, c
        )

    def fwd_arrival(t, c):
        return remote(fwd_buf.at[t, c], rows_buf.at[t, c], f_send.at[t, c], f_recv.at[t, c], row_me, c)

    def relay(t):
        codes = code_recv[t][0:1, :].astype(jnp.int32)
        choose = one_hot(iota((CK, Q), 0) + 1 == codes)
        fwd_buf[t] = mm(choose, chunk_buf[t]).astype(BF16).reshape(C, K, D)
        for d in range(1, C):
            fwd_copy(t, lax.rem(col_me + d, C)).start()
        rows_buf[t, col_me] = fwd_buf[t, col_me]

    def absorb(t):
        for d in range(1, C):
            fwd_arrival(t, lax.rem(col_me + d, C)).wait_recv()
        mine = rows_buf[t].reshape(CK, D)
        column = tag_col[t]
        line = tag_row[t]
        gram = mm_t(mine, mine)
        diag = jnp.where(eye, gram, 0.0)
        scale = lax.rsqrt(jnp.sum(diag, axis=1, keepdims=True) + 1.0)
        inv_col[t] = scale
        inv_row[t] = lax.rsqrt(jnp.sum(diag, axis=0, keepdims=True) + 1.0)
        member = iota((CK, S), 1).astype(F32) == column - 1.0
        cross = mm_t(mine, cent_ref[...]) * cent_inv
        similarity = jnp.sum(jnp.where(member, cross, 0.0), axis=1, keepdims=True) * scale
        sim_col[t] = similarity
        stats_ref[0:1, :] += jnp.sum(jnp.where(member, 1.0, 0.0), axis=0, keepdims=True)
        stats_ref[1:2, :] += jnp.sum(jnp.where(member, similarity, 0.0), axis=0, keepdims=True)
        stats_ref[2:3, :] += jnp.sum(
            jnp.where(member, similarity * similarity, 0.0), axis=0, keepdims=True
        )
        same = (column == line) & jnp.logical_not(eye)
        best = jnp.max(jnp.where(same, gram * scale, 0.0), axis=0, keepdims=True)

        def pair(u, best):
            other = rows_buf[u].reshape(CK, D)
            down = mm_t(other, mine)
            up = mm_t(mine, other)
            from_other = jnp.where(tag_col[u] == line, down * inv_col[u], 0.0)
            from_mine = jnp.where(column == tag_row[u], up * scale, 0.0)
            best_row[u] = jnp.maximum(best_row[u], jnp.max(from_mine, axis=0, keepdims=True))
            return jnp.maximum(best, jnp.max(from_other, axis=0, keepdims=True))

        best_row[t] = lax.fori_loop(0, t, pair, best)

    relay(0)

    def advance(t, carry):
        for copy in send_copy(t):
            copy.wait_recv()
        relay(t)
        absorb(t - 1)
        return carry

    lax.fori_loop(1, R, advance, 0)
    absorb(R - 1)

    floor = jnp.maximum(stats_ref[0:1, :], 1.0)
    mean = stats_ref[1:2, :] / floor
    variance = jnp.maximum(stats_ref[2:3, :] / floor - mean * mean, 0.0)
    spread_inv = 1.0 / jnp.sqrt(variance + 1.0 / D)

    def res_copy(q):
        t, r, c = peer(q)
        return remote(res_send.at[t * C + c], res_recv.at[own], r_send.at[q], r_recv.at[own], r, c)

    def res_arrival(q):
        t, r, c = peer(q)
        o = r * C + c
        return remote(res_send.at[t * C + c], res_recv.at[o], r_send.at[q], r_recv.at[o], r, c)

    half = LANES // 2

    def finish(t, carry):
        column = tag_col[t]
        member = iota((CK, S), 1).astype(F32) == column - 1.0
        centre = jnp.sum(jnp.where(member, mean, 0.0), axis=1, keepdims=True)
        width = jnp.sum(jnp.where(member, spread_inv, 0.0), axis=1, keepdims=True)
        proto = (centre - sim_col[t]) * width
        flat = best_row[t] * inv_row[t] * math.sqrt(D)
        redundant = jnp.sum(jnp.where(eye, flat, 0.0), axis=1, keepdims=True)
        lane = iota((CK, LANES), 1)
        rank = lax.rem(iota((CK, LANES), 0), K)
        lined = jnp.where(lane == rank, proto, 0.0) + jnp.where(lane == rank + half, redundant, 0.0)
        gather = lax.shift_right_logical(iota((C * SUB, CK), 0), 3) == lax.div(iota((C * SUB, CK), 1), K)
        packed = lax.dot_general(
            jnp.where(gather, 1.0, 0.0),
            lined,
            (((1,), (0,)), ((), ())),
            precision=HIGH,
            preferred_element_type=F32,
        )
        res_send[pl.ds(t * C, C)] = packed.reshape(C, SUB, LANES)
        return carry

    lax.fori_loop(0, R, finish, 0)

    def start_res(q, carry):
        res_copy(q).start()
        return carry

    lax.fori_loop(1, O, start_res, 0)
    res_recv[own] = res_send[col_me]

    def drain(t, carry):
        for copy in send_copy(t):
            copy.wait_send()
        return carry

    lax.fori_loop(1, R, drain, 0)

    def drain_fwd(t, carry):
        for d in range(1, C):
            fwd_copy(t, lax.rem(col_me + d, C)).wait_send()
        return carry

    lax.fori_loop(0, R, drain_fwd, 0)

    def drain_small(q, carry):
        tbl_copy(q).wait_send()
        res_copy(q).wait_send()
        return carry

    lax.fori_loop(1, O, drain_small, 0)

    def wait_res(q, carry):
        res_arrival(q).wait_recv()
        return carry

    lax.fori_loop(1, O, wait_res, 0)

    results = res_recv[...].reshape(O * SUB, LANES).T
    pick_owner = jnp.where(iota((O * SUB, L), 0) == owner_i * SUB, 1.0, 0.0)
    found = lax.dot_general(
        results, pick_owner, (((1,), (0,)), ((), ())), precision=HIGH, preferred_element_type=F32
    )
    sublane = iota((LANES, L), 0)
    proto_ref[...] = jnp.sum(jnp.where(sublane == rank_i, found, 0.0), axis=0, keepdims=True)
    red_ref[...] = jnp.sum(jnp.where(sublane == rank_i + half, found, 0.0), axis=0, keepdims=True)


def local(documents, assigned, centroids, owner_slot):
    L, D = documents.shape
    S = centroids.shape[0]
    R = lax.axis_size("dp")
    C = lax.axis_size("cent")
    O = R * C
    pair_cap = 2 * L // O
    row_cap = 5 * C * pair_cap // 8
    K = round_up(pair_cap, 16)
    Q = round_up(row_cap, 16)
    CK = C * K
    vmem = pl.BlockSpec(memory_space=pltpu.VMEM)
    dma = pltpu.SemaphoreType.DMA
    proto, red, stats = pl.pallas_call(
        functools.partial(kernel, (R, C, K, Q)),
        name="cluster_exchange",
        out_shape=(
            jax.ShapeDtypeStruct((1, L), F32),
            jax.ShapeDtypeStruct((1, L), F32),
            jax.ShapeDtypeStruct((3, S), F32),
        ),
        in_specs=[vmem] * 4,
        out_specs=(vmem, vmem, vmem),
        scratch_shapes=[
            pltpu.VMEM((R, Q, D), BF16),
            pltpu.VMEM((R, Q, D), BF16),
            pltpu.VMEM((R, SUB, Q), F32),
            pltpu.VMEM((R, SUB, Q), F32),
            pltpu.VMEM((R, C, K, D), BF16),
            pltpu.VMEM((R, C, K, D), BF16),
            pltpu.VMEM((O, SUB, LANES), F32),
            pltpu.VMEM((O, SUB, LANES), F32),
            pltpu.VMEM((O, SUB, LANES), F32),
            pltpu.VMEM((O, SUB, LANES), F32),
            pltpu.VMEM((SUB, L), jnp.int32),
            pltpu.VMEM((R, CK, 1), F32),
            pltpu.VMEM((R, 1, CK), F32),
            pltpu.VMEM((R, CK, 1), F32),
            pltpu.VMEM((R, 1, CK), F32),
            pltpu.VMEM((R, CK, 1), F32),
            pltpu.VMEM((R, 1, CK), F32),
            dma((R,)),
            dma((R,)),
            dma((R,)),
            dma((R,)),
            dma((R, C)),
            dma((R, C)),
            dma((O,)),
            dma((O,)),
            dma((O,)),
            dma((O,)),
        ],
        compiler_params=pltpu.CompilerParams(
            collective_id=0, has_side_effects=True, vmem_limit_bytes=62 * 1024 * 1024
        ),
    )(
        documents,
        assigned.reshape(1, L),
        centroids,
        owner_slot.reshape(-1, LANES),
    )
    return proto.reshape(L), red.reshape(L), stats


def solution(mesh):
    in_specs = (P(("dp", "cent"), None), P(("dp", "cent")), P(("dp", "cent"), None), P())
    out_specs = (P(("dp", "cent")), P(("dp", "cent")), P(None, ("dp", "cent")))
    return jax.shard_map(local, mesh=mesh, in_specs=in_specs, out_specs=out_specs, check_vma=False)
```

time: 224 us -> 141 us (0.63)
  Pallas kernels: 0 us -> 137 us
  waiting for transfers between devices: 92.9 us -> 0 us
  local copies, waits for them, and re-layouts: 67.8 us -> 3.76 us
  starting transfers between devices: 31.7 us -> 0 us
  other arithmetic: 10.4 us -> 0 us
  blocking collectives: 9.92 us -> 0 us
  matrix products: 9.77 us -> 0 us
    pallas_call x0 -> x1, Pallas kernels: none -> 137 us  [local(): pl.pallas_call(functools.partial(kernel, (R, C, K, Q)), name='cluster_exc...]
    all_to_all x7 -> x0, waiting for transfers between devices: 92.9 us -> none  [the longest x1 52 us: local(): lax.all_to_all(outgoing.reshape(dp_count, row_cap, width), 'dp', split_ax...]
    gather x11 -> x0, local copies, waits for them, and re-layouts: 42.4 us -> none  [the longest x1 6.87 us: owner_work(): mean_sim[safe_slot] - similarity]
    all_to_all x7 -> x0, starting transfers between devices: 31.7 us -> none  [the longest x1 7.28 us: local(): lax.all_to_all(tag_ids.reshape(dp_count, row_cap), 'dp', split_axis=0, co...]
    scatter x4 -> x0, local copies, waits for them, and re-layouts: 22.9 us -> none  [the longest x1 9.4 us: local(): forward = jnp.zeros((cent_count * inner_cap, width), jnp.bfloat16).at[sec...]
    all_to_all x1 -> x0, blocking collectives: 9.92 us -> none  [local(): lax.all_to_all(relay_redundant.reshape(dp_count, row_cap), 'dp', split_ax...]
    dot_general x4 -> x0, matrix products: 9.77 us -> none  [the longest x1 8.54 us: owner_work(): lax.dot_general(incoming, incoming, (((1,), (1,)), ((), ())), preferred_e...]
    dot_general x2 -> x0, other arithmetic: 5.58 us -> none  [the longest x1 5.2 us: owner_work(): jnp.einsum('sd,sd->s', incoming, incoming, preferred_element_type=jnp.flo...]
  transfers between devices with their start and end apart: 7 -> 0, of which waited for: 4 -> 0; matrix products, arithmetic and copies ran while one was open for 22% -> 0% of each run, Pallas kernels for 0% -> 0%
where the time goes in v1:
time: 141 us
  Pallas kernels  137 us (97%)
  local copies, waits for them, and re-layouts  3.76 us (3%)
    pallas_call x1, Pallas kernels, local(): pl.pallas_call(functools.partial(kernel, (R, C, K, Q)), name='cluster_exc...  137 us
    unnamed x3, local copies, waits for them, and re-layouts  3.76 us

profile of v1, /device:TPU:0, one launch (start us, length us, event | category | flops | bytes accessed | tf_op | source)
XLA Modules:
  0.0 141.0 jit_solution(13343025945549310352)
XLA Ops:
  0.6 136.6 %cluster_exchange.1 = (f32[1,512]{1,0:T(1,128)}, f32[1,512]{1,0:T(1,128)}, f32[3,384]{1,0:T(4,128)}) custom-call(bf16[512,2048]{1,0:T(8,128)(2,1)} %docs_ref.1, s32[1,512]{1,0:T(1,128)} %bitcast.5, bf16[384,2048]{1,0:T(8,128)(2,1)} %cent_ref.1, s32[96,128]{1,0:T(8,128)} %bitcast.4), custom_call_target="tpu_custom_call" | custom-call | tf_op jit(solution)/shard_map/cluster_exchange/pallas_call | solution.py:409
  137.2 1.2 copy.10
  138.5 1.2 copy.11
  139.7 1.3 copy.12

commit v2 on v1

--- a/solution.py
+++ b/solution.py
@@ -19,13 +19,12 @@
     return -(-value // unit) * unit
 
 
-def exclusive_or(left, right, extent):
-    total = 0
-    bit = 1
-    while bit < extent:
-        total = total + lax.rem(lax.rem(lax.div(left, bit), 2) + lax.rem(lax.div(right, bit), 2), 2) * bit
-        bit *= 2
-    return total
+def each(low, high, body):
+    if high - low <= 8:
+        for step in range(low, high):
+            body(step)
+    else:
+        lax.fori_loop(low, high, lambda step, carry: (body(step), carry)[1], 0)
 
 
 def iota(shape, dim):
@@ -63,7 +62,6 @@
     tbl_recv,
     res_send,
     res_recv,
-    pos_buf,
     tag_col,
     tag_row,
     inv_col,
@@ -91,9 +89,30 @@
     col_me = lax.axis_index("cent")
     own = row_me * C + col_me
 
-    def peer(q):
-        step = lax.div(q, C)
-        return step, exclusive_or(row_me, step, R), lax.rem(col_me + lax.rem(q, C), C)
+    bits = []
+    while 2 ** len(bits) < R:
+        bits.append(lax.rem(lax.div(row_me, 2 ** len(bits)), 2))
+    col_of = [col_me] + [lax.rem(col_me + d, C) for d in range(1, C)]
+
+    def row_of(t):
+        total = 0
+        for i, bit in enumerate(bits):
+            if isinstance(t, int):
+                total = total + (1 - bit if (t >> i) & 1 else bit) * 2**i
+            else:
+                total = total + lax.rem(bit + lax.div(t, 2**i), 2) * 2**i
+        return total
+
+    def all_peers(body):
+        for d in range(1, C):
+            body(0, row_me, d)
+
+        def at_row(t):
+            r = row_of(t)
+            for d in range(C):
+                body(t, r, d)
+
+        each(1, R, at_row)
 
     def where_is(r, c):
         return {"dp": r, "cent": c}
@@ -110,14 +129,12 @@
 
     barrier = pltpu.get_barrier_semaphore()
 
-    def greet(q, carry):
-        _, r, c = peer(q)
+    def greet(t, r, d):
         pl.semaphore_signal(
-            barrier, inc=1, device_id=where_is(r, c), device_id_type=pl.DeviceIdType.MESH
-        )
-        return carry
-
-    lax.fori_loop(1, O, greet, 0)
+            barrier, inc=1, device_id=where_is(r, col_of[d]), device_id_type=pl.DeviceIdType.MESH
+        )
+
+    all_peers(greet)
 
     assigned = assigned_ref[...]
     high = lax.shift_right_logical(assigned, 7)
@@ -145,11 +162,11 @@
     earlier = one_hot(iota((L, L), 0) < iota((L, L), 1))
     rank_owner = jnp.sum(mm(is_owner.astype(BF16), earlier) * is_owner, axis=0, keepdims=True)
     rank_row = jnp.sum(mm(is_row.astype(BF16), earlier) * is_row, axis=0, keepdims=True)
-    position = (row * Q + rank_row).astype(jnp.int32)
+    position = jnp.bitwise_xor(row_i, row_me) * Q + rank_row.astype(jnp.int32)
     code = ((owner - row * C) * K + rank_owner + 1.0).astype(BF16)
     code8 = jnp.broadcast_to(code, (SUB, L))
     rank_i = rank_owner.astype(jnp.int32)
-    pos_buf[...] = jnp.broadcast_to(position, (SUB, L))
+    docs = docs_ref[...]
 
     is_owner8 = lax.shift_right_logical(iota((O * SUB, L), 0), 3) == owner_i
     is_rank = one_hot(iota((LANES, L), 0) == rank_i)
@@ -163,51 +180,67 @@
 
     pl.semaphore_wait(barrier, O - 1)
 
-    def send_copy(t):
-        r = exclusive_or(row_me, t, R)
-        return (
-            remote(send_buf.at[t], chunk_buf.at[t], a_send.at[t], a_recv.at[t], r, col_me),
-            remote(code_send.at[t], code_recv.at[t], m_send.at[t], m_recv.at[t], r, col_me),
-        )
-
-    def bucket(t):
-        r = exclusive_or(row_me, t, R)
-        choose = one_hot(iota((Q, L), 0) + r * Q == pos_buf[0:1, :])
-        return mm(choose, docs_ref[...]).astype(BF16), mm_t(code8, choose)
-
-    def ship(t, carry):
-        packed, codes = bucket(t)
-        send_buf[t] = packed
-        code_send[t] = codes
-        for copy in send_copy(t):
-            copy.start()
-        return carry
-
-    lax.fori_loop(1, R, ship, 0)
-    packed, codes = bucket(0)
-    chunk_buf[0] = packed
-    code_recv[0] = codes
-
-    def tbl_copy(q):
-        t, r, c = peer(q)
+    def tbl_copy(t, r, d):
         return remote(
-            tbl_send.at[r * C + c], tbl_recv.at[t * C + col_me], t_send.at[q], t_recv.at[t * C + col_me], r, c
-        )
-
-    def tbl_arrival(q):
-        t, r, c = peer(q)
+            tbl_send.at[r * C + col_of[d]],
+            tbl_recv.at[t * C + col_me],
+            t_send.at[t * C + d],
+            t_recv.at[t * C + col_me],
+            r,
+            col_of[d],
+        )
+
+    def tbl_arrival(t, r, d):
         return remote(
-            tbl_send.at[r * C + c], tbl_recv.at[t * C + c], t_send.at[q], t_recv.at[t * C + c], r, c
-        )
-
-    def start_tbl(q, carry):
-        tbl_copy(q).start()
-        return carry
-
-    lax.fori_loop(1, O, start_tbl, 0)
+            tbl_send.at[r * C + col_of[d]],
+            tbl_recv.at[t * C + col_of[d]],
+            t_send.at[t * C + d],
+            t_recv.at[t * C + col_of[d]],
+            r,
+            col_of[d],
+        )
+
+    all_peers(lambda t, r, d: tbl_copy(t, r, d).start())
     tbl_recv[col_me] = tbl_send[own]
 
-    cent_sq = jnp.zeros((SUB, S), F32)
+    def row_copy(t, r):
+        return remote(send_buf.at[t], chunk_buf.at[t], a_send.at[t], a_recv.at[t], r, col_me)
+
+    def code_copy(t, r):
+        return remote(code_send.at[t], code_recv.at[t], m_send.at[t], m_recv.at[t], r, col_me)
+
+    def mark(t):
+        code_send[t] = mm_t(code8, one_hot(iota((Q, L), 0) + t * Q == position))
+
+    each(0, R, mark)
+    each(1, R, lambda t: code_copy(t, row_of(t)).start())
+    code_recv[0] = code_send[0]
+
+    group = max(1, R // 2)
+    for first in range(0, R, group):
+        choose = one_hot(iota((group * Q, L), 0) + first * Q == position)
+        send_buf[first : first + group] = mm(choose, docs).astype(BF16).reshape(group, Q, D)
+        each(max(first, 1), first + group, lambda t: row_copy(t, row_of(t)).start())
+    chunk_buf[0] = send_buf[0]
+
+    def fwd_copy(t, c):
+        return remote(
+            fwd_buf.at[t, c], rows_buf.at[t, col_me], f_send.at[t, c], f_recv.at[t, col_me], row_me, c
+        )
+
+    def fwd_arrival(t, c):
+        return remote(fwd_buf.at[t, c], rows_buf.at[t, c], f_send.at[t, c], f_recv.at[t, c], row_me, c)
+
+    def relay(t):
+        codes = code_recv[t][0:1, :].astype(jnp.int32)
+        choose = one_hot(iota((CK, Q), 0) + 1 == codes)
+        fwd_buf[t] = mm(choose, chunk_buf[t]).astype(BF16).reshape(C, K, D)
+        for d in range(1, C):
+            fwd_copy(t, col_of[d]).start()
+        rows_buf[t, col_me] = fwd_buf[t, col_me]
+
+    relay(0)
+
     ones = jnp.ones((SUB, 256), F32)
 
     squares = []
@@ -223,11 +256,7 @@
     )
     cent_inv = lax.rsqrt(cent_sq[0:1, :] + 1.0)
 
-    def wait_tbl(q, carry):
-        tbl_arrival(q).wait_recv()
-        return carry
-
-    lax.fori_loop(1, O, wait_tbl, 0)
+    all_peers(lambda t, r, d: tbl_arrival(t, r, d).wait_recv())
 
     eye = iota((CK, CK), 0) == iota((CK, CK), 1)
 
@@ -247,25 +276,9 @@
 
     stats_ref[...] = jnp.zeros(stats_ref.shape, F32)
 
-    def fwd_copy(t, c):
-        return remote(
-            fwd_buf.at[t, c], rows_buf.at[t, col_me], f_send.at[t, c], f_recv.at[t, col_me], row_me, c
-        )
-
-    def fwd_arrival(t, c):
-        return remote(fwd_buf.at[t, c], rows_buf.at[t, c], f_send.at[t, c], f_recv.at[t, c], row_me, c)
-
-    def relay(t):
-        codes = code_recv[t][0:1, :].astype(jnp.int32)
-        choose = one_hot(iota((CK, Q), 0) + 1 == codes)
-        fwd_buf[t] = mm(choose, chunk_buf[t]).astype(BF16).reshape(C, K, D)
-        for d in range(1, C):
-            fwd_copy(t, lax.rem(col_me + d, C)).start()
-        rows_buf[t, col_me] = fwd_buf[t, col_me]
-
     def absorb(t):
         for d in range(1, C):
-            fwd_arrival(t, lax.rem(col_me + d, C)).wait_recv()
+            fwd_arrival(t, col_of[d]).wait_recv()
         mine = rows_buf[t].reshape(CK, D)
         column = tag_col[t]
         line = tag_row[t]
@@ -297,11 +310,9 @@
 
         best_row[t] = lax.fori_loop(0, t, pair, best)
 
-    relay(0)
-
     def advance(t, carry):
-        for copy in send_copy(t):
-            copy.wait_recv()
+        code_copy(t, row_of(R - 1)).wait_recv()
+        row_copy(t, row_of(R - 1)).wait_recv()
         relay(t)
         absorb(t - 1)
         return carry
@@ -314,14 +325,21 @@
     variance = jnp.maximum(stats_ref[2:3, :] / floor - mean * mean, 0.0)
     spread_inv = 1.0 / jnp.sqrt(variance + 1.0 / D)
 
-    def res_copy(q):
-        t, r, c = peer(q)
-        return remote(res_send.at[t * C + c], res_recv.at[own], r_send.at[q], r_recv.at[own], r, c)
-
-    def res_arrival(q):
-        t, r, c = peer(q)
-        o = r * C + c
-        return remote(res_send.at[t * C + c], res_recv.at[o], r_send.at[q], r_recv.at[o], r, c)
+    def res_copy(t, r, d):
+        return remote(
+            res_send.at[t * C + col_of[d]],
+            res_recv.at[own],
+            r_send.at[t * C + d],
+            r_recv.at[own],
+            r,
+            col_of[d],
+        )
+
+    def res_arrival(t, r, d):
+        o = r * C + col_of[d]
+        return remote(
+            res_send.at[t * C + col_of[d]], res_recv.at[o], r_send.at[t * C + d], r_recv.at[o], r, col_of[d]
+        )
 
     half = LANES // 2
 
@@ -349,39 +367,27 @@
 
     lax.fori_loop(0, R, finish, 0)
 
-    def start_res(q, carry):
-        res_copy(q).start()
-        return carry
-
-    lax.fori_loop(1, O, start_res, 0)
+    all_peers(lambda t, r, d: res_copy(t, r, d).start())
     res_recv[own] = res_send[col_me]
 
-    def drain(t, carry):
-        for copy in send_copy(t):
-            copy.wait_send()
-        return carry
-
-    lax.fori_loop(1, R, drain, 0)
-
-    def drain_fwd(t, carry):
+    def drain(t):
+        code_copy(t, row_of(t)).wait_send()
+        row_copy(t, row_of(t)).wait_send()
+
+    each(1, R, drain)
+
+    def drain_fwd(t):
         for d in range(1, C):
-            fwd_copy(t, lax.rem(col_me + d, C)).wait_send()
-        return carry
-
-    lax.fori_loop(0, R, drain_fwd, 0)
-
-    def drain_small(q, carry):
-        tbl_copy(q).wait_send()
-        res_copy(q).wait_send()
-        return carry
-
-    lax.fori_loop(1, O, drain_small, 0)
-
-    def wait_res(q, carry):
-        res_arrival(q).wait_recv()
-        return carry
-
-    lax.fori_loop(1, O, wait_res, 0)
+            fwd_copy(t, col_of[d]).wait_send()
+
+    each(0, R, drain_fwd)
+
+    def drain_small(t, r, d):
+        tbl_copy(t, r, d).wait_send()
+        res_copy(t, r, d).wait_send()
+
+    all_peers(drain_small)
+    all_peers(lambda t, r, d: res_arrival(t, r, d).wait_recv())
 
     results = res_recv[...].reshape(O * SUB, LANES).T
     pick_owner = jnp.where(iota((O * SUB, L), 0) == owner_i * SUB, 1.0, 0.0)
@@ -427,7 +433,6 @@
             pltpu.VMEM((O, SUB, LANES), F32),
             pltpu.VMEM((O, SUB, LANES), F32),
             pltpu.VMEM((O, SUB, LANES), F32),
-            pltpu.VMEM((SUB, L), jnp.int32),
             pltpu.VMEM((R, CK, 1), F32),
             pltpu.VMEM((R, 1, CK), F32),
             pltpu.VMEM((R, CK, 1), F32),

time: 141 us -> 96.7 us (0.69)
  Pallas kernels: 137 us -> 92.1 us
    pallas_call x1, Pallas kernels: 137 us -> 92.1 us  [local(): pl.pallas_call(functools.partial(kernel, (R, C, K, Q)), name='cluster_exc...]
where the time goes in v2:
time: 96.7 us; the launch traced here: 96.5 us
  Pallas kernels  92.1 us (95%)
  local copies, waits for them, and re-layouts  3.76 us (4%)
    pallas_call x1, Pallas kernels, local(): pl.pallas_call(functools.partial(kernel, (R, C, K, Q)), name='cluster_exc...  92.1 us
    unnamed x3, local copies, waits for them, and re-layouts  3.76 us

profile of v2, /device:TPU:0, one launch (start us, length us, event | category | flops | bytes accessed | tf_op | source)
XLA Modules:
  0.0 96.5 jit_solution(15967316334999124824)
XLA Ops:
  0.6 92.1 %cluster_exchange.1 = (f32[1,512]{1,0:T(1,128)}, f32[1,512]{1,0:T(1,128)}, f32[3,384]{1,0:T(4,128)}) custom-call(bf16[512,2048]{1,0:T(8,128)(2,1)} %docs_ref.1, s32[1,512]{1,0:T(1,128)} %bitcast.5, bf16[384,2048]{1,0:T(8,128)(2,1)} %cent_ref.1, s32[96,128]{1,0:T(8,128)} %bitcast.4), custom_call_target="tpu_custom_call" | custom-call | tf_op jit(solution)/shard_map/cluster_exchange/pallas_call | solution.py:415
  92.7 1.2 %copy.10 = f32[512]{0:T(512)} copy(f32[512]{0:T(512)} %bitcast.7) | data formatting | bytes 4096
  94.0 1.2 %copy.11 = f32[512]{0:T(512)} copy(f32[512]{0:T(512)} %bitcast.6) | data formatting | bytes 4096
  95.2 1.3 %copy.12 = f32[3,384]{1,0:T(4,128)} copy(f32[3,384]{1,0:T(4,128)} %get-tuple-element.14) | data formatting | bytes 9216

commit v3 on v2

--- a/solution.py
+++ b/solution.py
@@ -49,9 +49,7 @@
     assigned_ref,
     cent_ref,
     table_ref,
-    proto_ref,
-    red_ref,
-    stats_ref,
+    out_ref,
     send_buf,
     chunk_buf,
     code_send,
@@ -78,6 +76,7 @@
     t_recv,
     r_send,
     r_recv,
+    stats_ref,
 ):
     R, C, K, Q = dims
     O = R * C
@@ -260,7 +259,7 @@
 
     eye = iota((CK, CK), 0) == iota((CK, CK), 1)
 
-    def spread(t, carry):
+    def spread(t):
         column = jnp.zeros((CK, 1), F32)
         for c in range(C):
             line = tbl_recv[t * C + c][0:1, :]
@@ -270,9 +269,8 @@
         tag_col[t] = column
         flat = jnp.sum(jnp.where(eye, column, 0.0), axis=0, keepdims=True)
         tag_row[t] = jnp.where(flat > 0.0, flat, -1.0)
-        return carry
-
-    lax.fori_loop(0, R, spread, 0)
+
+    each(0, R, spread)
 
     stats_ref[...] = jnp.zeros(stats_ref.shape, F32)
 
@@ -323,6 +321,7 @@
     floor = jnp.maximum(stats_ref[0:1, :], 1.0)
     mean = stats_ref[1:2, :] / floor
     variance = jnp.maximum(stats_ref[2:3, :] / floor - mean * mean, 0.0)
+    out_ref[2:5, :S] = stats_ref[...]
     spread_inv = 1.0 / jnp.sqrt(variance + 1.0 / D)
 
     def res_copy(t, r, d):
@@ -343,7 +342,7 @@
 
     half = LANES // 2
 
-    def finish(t, carry):
+    def finish(t):
         column = tag_col[t]
         member = iota((CK, S), 1).astype(F32) == column - 1.0
         centre = jnp.sum(jnp.where(member, mean, 0.0), axis=1, keepdims=True)
@@ -363,11 +362,17 @@
             preferred_element_type=F32,
         )
         res_send[pl.ds(t * C, C)] = packed.reshape(C, SUB, LANES)
-        return carry
-
-    lax.fori_loop(0, R, finish, 0)
-
-    all_peers(lambda t, r, d: res_copy(t, r, d).start())
+
+    def deliver(t):
+        finish(t)
+        r = row_of(t)
+        for d in range(C):
+            res_copy(t, r, d).start()
+
+    each(1, R, deliver)
+    finish(0)
+    for d in range(1, C):
+        res_copy(0, row_me, d).start()
     res_recv[own] = res_send[col_me]
 
     def drain(t):
@@ -395,8 +400,8 @@
         results, pick_owner, (((1,), (0,)), ((), ())), precision=HIGH, preferred_element_type=F32
     )
     sublane = iota((LANES, L), 0)
-    proto_ref[...] = jnp.sum(jnp.where(sublane == rank_i, found, 0.0), axis=0, keepdims=True)
-    red_ref[...] = jnp.sum(jnp.where(sublane == rank_i + half, found, 0.0), axis=0, keepdims=True)
+    out_ref[0:1, :L] = jnp.sum(jnp.where(sublane == rank_i, found, 0.0), axis=0, keepdims=True)
+    out_ref[1:2, :L] = jnp.sum(jnp.where(sublane == rank_i + half, found, 0.0), axis=0, keepdims=True)
 
 
 def local(documents, assigned, centroids, owner_slot):
@@ -412,16 +417,12 @@
     CK = C * K
     vmem = pl.BlockSpec(memory_space=pltpu.VMEM)
     dma = pltpu.SemaphoreType.DMA
-    proto, red, stats = pl.pallas_call(
+    packed = pl.pallas_call(
         functools.partial(kernel, (R, C, K, Q)),
         name="cluster_exchange",
-        out_shape=(
-            jax.ShapeDtypeStruct((1, L), F32),
-            jax.ShapeDtypeStruct((1, L), F32),
-            jax.ShapeDtypeStruct((3, S), F32),
-        ),
+        out_shape=jax.ShapeDtypeStruct((SUB, max(L, S)), F32),
         in_specs=[vmem] * 4,
-        out_specs=(vmem, vmem, vmem),
+        out_specs=vmem,
         scratch_shapes=[
             pltpu.VMEM((R, Q, D), BF16),
             pltpu.VMEM((R, Q, D), BF16),
@@ -449,6 +450,7 @@
             dma((O,)),
             dma((O,)),
             dma((O,)),
+            pltpu.VMEM((3, S), F32),
         ],
         compiler_params=pltpu.CompilerParams(
             collective_id=0, has_side_effects=True, vmem_limit_bytes=62 * 1024 * 1024
@@ -459,7 +461,7 @@
         centroids,
         owner_slot.reshape(-1, LANES),
     )
-    return proto.reshape(L), red.reshape(L), stats
+    return packed[0, :L], packed[1, :L], packed[2:5, :S]
 
 
 def solution(mesh):

time: 96.7 us -> 94.7 us (0.979)
  Pallas kernels: 92.1 us -> 90.9 us
  local copies, waits for them, and re-layouts: 3.76 us -> 2.68 us
    unnamed x3 -> x0, local copies, waits for them, and re-layouts: 3.76 us -> none
    slice x0 -> x2, local copies, waits for them, and re-layouts: none -> 2.68 us  [local(): return (packed[0, :L], packed[1, :L], packed[2:5, :S])]
    pallas_call x1, Pallas kernels: 92.1 us -> 90.9 us  [local(): pl.pallas_call(functools.partial(kernel, (R, C, K, Q)), name='cluster_exc...]
where the time goes in v3:
time: 94.7 us; the launch traced here: 94.3 us
  Pallas kernels  90.9 us (96%)
  local copies, waits for them, and re-layouts  2.68 us (3%)
    pallas_call x1, Pallas kernels, local(): pl.pallas_call(functools.partial(kernel, (R, C, K, Q)), name='cluster_exc...  90.9 us
    slice x2, local copies, waits for them, and re-layouts, local(): return (packed[0, :L], packed[1, :L], packed[2:5, :S])  2.68 us

profile of v3, /device:TPU:0, one launch (start us, length us, event | category | flops | bytes accessed | tf_op | source)
XLA Modules:
  0.0 94.3 jit_solution(12000887121356180778)
XLA Ops:
  0.6 90.9 %cluster_exchange.1 = f32[8,512]{1,0:T(8,128)} custom-call(bf16[512,2048]{1,0:T(8,128)(2,1)} %docs_ref.1, s32[1,512]{1,0:T(1,128)} %bitcast.5, bf16[384,2048]{1,0:T(8,128)(2,1)} %cent_ref.1, s32[96,128]{1,0:T(8,128)} %bitcast.4), custom_call_target="tpu_custom_call" | custom-call | tf_op jit(solution)/shard_map/cluster_exchange/pallas_call | solution.py:420
  91.6 1.4 %fusion = (f32[1,512]{1,0:T(1,128)}, f32[1,512]{1,0:T(1,128)}) fusion(f32[8,512]{1,0:T(8,128)} %cluster_exchange.1), kind=kLoop, calls=%fused_computation | loop fusion | bytes 8192 | tf_op jit(solution)/shard_map/slice | solution.py:464
  93.0 1.3 %slice.11 = f32[3,384]{1,0:T(4,128)} slice(f32[8,512]{1,0:T(8,128)} %cluster_exchange.1), slice={[2:5], [0:384]} | slice | bytes 9216 | tf_op jit(solution)/shard_map/slice | solution.py:464
